TPU v7x, 128 devices: a whole 4x4x4 slice. The times are simulated.
128 devices in a mesh: dp: 8 (over z_hi, x), expert: 16 (over y, z_lo, core).
Axes of the slice: x: 4, y: 4, z: 4 (z_hi: 2, z_lo: 2; z = z_hi * 2 + z_lo), core: 2. Of those that a mesh axis runs over, the one named last changes fastest.
Arguments:
- tokens: bfloat16 [32768, 2048], P(('dp', 'expert')), may hold values from -6 to 6
- expert_ids: int32 [32768, 8], P(('dp', 'expert')), may hold values from 0 to 31, all different within a row; in each aligned block of 256 rows (0 to 255, 256 to 511, ...) at most 80 rows name the same one
- route_probs: float32 [32768, 8], P(('dp', 'expert')), may hold values from 0.05 to 1
- w_gate_up: bfloat16 [32, 2048, 1536], P('expert', 'dp'), may hold values from -0.125 to 0.125
- w_down: bfloat16 [32, 768, 2048], P('expert', None, 'dp'), may hold values from -0.21875 to 0.21875
Outputs:
- moe_out: bfloat16 [32768, 2048], P(('dp', 'expert'))
Inputs may be any that keep to these rules, and one draw needn't show every extreme that they name: `expert_ids`: each row names 8 different experts. Among the rows of one device no expert is named more than 80 times, and in every draw some expert is named exactly 80 times in some device's rows.
All inputs are finite; a program needn't handle non-finite values.
Results may differ from a plain program's by a relative error of at most 0.0057.
Values may be sent and summed in bfloat16 or wider, within the bound.
A program may use at most 128 MiB of HBM per device.

v0:
```python
import jax
import jax.numpy as jnp
from jax import lax
from jax.sharding import Mesh
from jax.sharding import PartitionSpec as P

DP = ("dp_0", "dp_1")
DP_EXPERT = ("dp_0", "dp_1", "expert")


def joined_along(pieces, dim):
    pieces = jnp.moveaxis(pieces, 0, dim)
    shape = pieces.shape
    return pieces.reshape(*shape[:dim], shape[dim] * shape[dim + 1], *shape[dim + 2 :])


def gather_in_order(array, axes, sequence):
    pieces = array
    for k in sequence:
        pieces = lax.all_gather(pieces, axes[k])
    done = sequence[::-1]
    back = [done.index(k) for k in range(len(axes))]
    pieces = pieces.transpose(*back, *range(len(axes), pieces.ndim))
    return pieces.reshape(-1, *array.shape)


def whole_of(array, axes, sequence, dim):
    return joined_along(gather_in_order(array, axes, sequence), dim)


def shards(tokens, expert_ids, route_probs, w_gate_up, w_down):
    owners = lax.axis_size("expert")
    local_count = w_gate_up.shape[0]
    experts = owners * local_count
    tok_rows = tokens.shape[0]
    model_width = tokens.shape[1]
    top_count = expert_ids.shape[1]
    capacity = 5 * tok_rows * top_count // (4 * experts)
    hidden_units = w_down.shape[1]
    flat_ids = expert_ids.reshape(-1)
    onehot = (flat_ids[:, None] == jnp.arange(experts, dtype=jnp.int32)[None, :]).astype(jnp.int32)
    before = jnp.cumsum(onehot, axis=0) - onehot
    slot_of = jnp.sum(before * onehot, axis=1)
    target = flat_ids * capacity + slot_of
    copies = jnp.repeat(tokens, top_count, axis=0)
    send_buffer = jnp.zeros((experts * capacity, model_width), jnp.bfloat16).at[target].set(copies)
    send_buffer = send_buffer.reshape(experts, capacity, model_width)
    received = lax.all_to_all(send_buffer, "expert", split_axis=0, concat_axis=1, tiled=True)
    returned_list = []
    for local_expert in range(local_count):
        rows_in = received[local_expert]
        joined = jnp.dot(
            rows_in,
            whole_of(w_gate_up[local_expert], DP, (0, 1), 0),
            preferred_element_type=jnp.float32,
        )
        hidden = (jax.nn.silu(joined[:, :hidden_units]) * joined[:, hidden_units:]).astype(
            jnp.bfloat16
        )
        returned_list.append(
            lax.all_to_all(
                jnp.dot(
                    hidden,
                    lax.all_gather(w_down[local_expert], DP, axis=1, tiled=True),
                    preferred_element_type=jnp.float32,
                ).astype(jnp.bfloat16),
                "expert",
                split_axis=0,
                concat_axis=0,
                tiled=True,
            )
        )
    returned = jnp.concatenate(returned_list, axis=0)
    source_rows = (
        flat_ids % local_count * (owners * capacity) + flat_ids // local_count * capacity + slot_of
    )
    gathered = returned[source_rows].reshape(tok_rows, top_count, model_width)
    weights = route_probs / jnp.sum(route_probs, axis=1, keepdims=True)
    combined = jnp.sum(gathered.astype(jnp.float32) * weights[:, :, None], axis=1)
    return combined.astype(jnp.bfloat16)


def solution(mesh):
    finer = Mesh(mesh.devices.reshape(2, 4, mesh.shape["expert"]), ("dp_0", "dp_1", "expert"))
    in_specs = (
        P(DP_EXPERT, None),
        P(DP_EXPERT, None),
        P(DP_EXPERT, None),
        P("expert", DP, None),
        P("expert", None, DP),
    )
    out_specs = P(DP_EXPERT, None)
    return jax.shard_map(
        shards, mesh=finer, in_specs=in_specs, out_specs=out_specs, check_vma=False
    )
```

profile of v0, /device:TPU:49, one launch (start us, length us, event | category | flops | bytes accessed | tf_op | source)
XLA Modules:
  0.0 568.1 jit_solution(15967926868259111235)
XLA Ops:
  6.5 2.8 fusion.23
  9.4 0.7 all-gather.13.cloned.1.call-update
  10.1 31.5 %all-gather.11.cloned.1.call-done = bf16[2,256,1536]{2,1,0:T(8,128)(2,1)} async-done(((bf16[1,256,1536]{2,1,0:T(8,128)(2,1)}), bf16[2,256,1536]{2,1,0:T(8,128)(2,1)}) %all-gather.11.cloned.1.call-update) | async-done | bytes 1572880 | tf_op jit(solution)/shard_map/all_gather | solution.py:20
  41.7 1.0 fusion.24
  43.2 9.1 %reduce-window.6 = s32[32,16,128]{2,1,0:T(8,128)S(1)} reduce-window(s32[32,16,128]{2,1,0:T(8,128)S(1)} %fusion.16, s32[]{:T(128)} %constant.38.clone.1), window={size=1x1x128 pad=0_0x0_0x127_0}, to_apply=%region_0.0 | reduce-window | flops 8323072 | bytes 524292 | tf_op jit(solution)/shard_map/reduce-window
  53.2 17.9 %scatter_custom_fusion = bf16[2560,2048]{1,0:T(8,128)(2,1)} fusion(s32[2048]{0:T(1024)S(1)} %bitcast.73, bf16[]{:T(256)} %constant.36.clone.1, bf16[256,2048]{1,0:T(8,128)(2,1)S(1)} %copy-done), kind=kCustom, calls=%fused_computation.5 | custom fusion | bytes 11534338 | tf_op jit(solution)/shard_map/scatter | solution.py:46
  71.1 6.4 %all-to-all-start = ((bf16[32,80,2048]{2,1,0:T(8,128)(2,1)}), bf16[32,80,2048]{2,1,0:T(8,128)(2,1)}, u32[]{:S(2)}, u32[]{:S(2)}) async-start(bf16[32,80,2048]{2,1,0:T(8,128)(2,1)} %bitcast.57), calls=%async_computation | async-start | bytes 20971520 | tf_op jit(solution)/shard_map/all_to_all | solution.py:48
  78.7 165.6 %all-to-all-done = bf16[32,80,2048]{2,1,0:T(8,128)(2,1)} async-done(((bf16[32,80,2048]{2,1,0:T(8,128)(2,1)}), bf16[32,80,2048]{2,1,0:T(8,128)(2,1)}, u32[]{:S(2)}, u32[]{:S(2)}) %all-to-all-start) | async-done | bytes 10485792 | tf_op jit(solution)/shard_map/all_to_all | solution.py:48
  244.3 10.1 %fusion.22 = (bf16[1,16,80,2048]{3,2,0,1:T(8,128)(2,1)}, bf16[1,16,80,2048]{3,2,0,1:T(8,128)(2,1)}) fusion(bf16[2,16,80,2048]{3,2,0,1:T(8,128)(2,1)} %bitcast.8), kind=kLoop, calls=%fused_computation.41 | loop fusion | bytes 20971520 | tf_op jit(solution)/shard_map/slice | solution.py:51
  254.4 3.6 copy.26
  258.0 0.7 copy-done.2
  258.7 10.6 %fusion.25 = f32[1280,1536]{1,0:T(8,128)} fusion(bf16[1280,2048]{1,0:T(8,128)(2,1)S(1)} %bitcast.65, bf16[2048,1536]{1,0:T(8,128)(2,1)S(1)} %bitcast.61), kind=kOutput, calls=%fused_computation.44 | convolution fusion | flops 8053063680 | bytes 19398656 | tf_op jit(solution)/shard_map/dot_general | solution.py:52
  269.3 10.9 %convolution_convert_fusion.1 = bf16[1280,2048]{1,0:T(8,128)(2,1)} fusion(bf16[1,768,2048]{2,1,0:T(8,128)(2,1)} %all-gather.17.cloned.1.call-done, f32[1280,1536]{1,0:T(8,128)} %fusion.25), kind=kOutput, calls=%fused_computation.8 | convolution fusion | flops 4035051520 | bytes 16252928 | tf_op jit(solution)/shard_map/dot_general | solution.py:62
  280.2 9.1 %all-to-all-start.1 = ((bf16[16,80,2048]{2,1,0:T(8,128)(2,1)}), bf16[16,80,2048]{2,1,0:T(8,128)(2,1)}, u32[]{:S(2)}, u32[]{:S(2)}) async-start(bf16[16,80,2048]{2,1,0:T(8,128)(2,1)} %bitcast.66), calls=%async_computation.1 | async-start | bytes 10485760 | tf_op jit(solution)/shard_map/all_to_all | solution.py:61
  289.3 48.6 %all-gather.19.cloned.1.call-done = bf16[8,256,1536]{2,1,0:T(8,128)(2,1)} async-done(((bf16[2,256,1536]{2,1,0:T(8,128)(2,1)}), bf16[8,256,1536]{2,1,0:T(8,128)(2,1)}) %all-gather.19.cloned.1.call-update) | async-done | bytes 6291472 | tf_op jit(solution)/shard_map/all_gather | solution.py:20
  337.9 3.6 copy.27
  341.9 10.5 %fusion.26 = f32[1280,1536]{1,0:T(8,128)} fusion(bf16[1280,2048]{1,0:T(8,128)(2,1)S(1)} %bitcast.64, bf16[2048,1536]{1,0:T(8,128)(2,1)S(1)} %bitcast.60), kind=kOutput, calls=%fused_computation.45 | convolution fusion | flops 8053063680 | bytes 19398656 | tf_op jit(solution)/shard_map/dot_general | solution.py:52
  352.5 63.8 %all-gather.21.cloned.1.call-done = bf16[1,768,2048]{2,1,0:T(8,128)(2,1)} async-done(((bf16[1,768,256]{2,1,0:T(8,128)(2,1)}), bf16[1,768,2048]{2,1,0:T(8,128)(2,1)}) %all-gather.21.cloned.1.call-update) | async-done | bytes 3145744 | tf_op jit(solution)/shard_map/all_gather | solution.py:64
  416.2 10.8 %convolution_convert_fusion = bf16[1280,2048]{1,0:T(8,128)(2,1)} fusion(bf16[1,768,2048]{2,1,0:T(8,128)(2,1)} %all-gather.21.cloned.1.call-done, f32[1280,1536]{1,0:T(8,128)} %fusion.26), kind=kOutput, calls=%fused_computation.7 | convolution fusion | flops 4035051520 | bytes 16252928 | tf_op jit(solution)/shard_map/dot_general | solution.py:62
  427.0 7.5 %all-to-all-start.2 = ((bf16[16,80,2048]{2,1,0:T(8,128)(2,1)}), bf16[16,80,2048]{2,1,0:T(8,128)(2,1)}, u32[]{:S(2)}, u32[]{:S(2)}) async-start(bf16[16,80,2048]{2,1,0:T(8,128)(2,1)} %bitcast.67), calls=%async_computation.2 | async-start | bytes 10485760 | tf_op jit(solution)/shard_map/all_to_all | solution.py:61
  434.7 79.5 %all-to-all-done.2 = bf16[16,80,2048]{2,1,0:T(8,128)(2,1)} async-done(((bf16[16,80,2048]{2,1,0:T(8,128)(2,1)}), bf16[16,80,2048]{2,1,0:T(8,128)(2,1)}, u32[]{:S(2)}, u32[]{:S(2)}) %all-to-all-start.2) | async-done | bytes 5242912 | tf_op jit(solution)/shard_map/all_to_all | solution.py:61
  514.2 12.7 %pad_maximum_fusion = bf16[2560,2048]{1,0:T(8,128)(2,1)} fusion(bf16[1280,2048]{1,0:T(8,128)(2,1)} %bitcast.23, bf16[1280,2048]{1,0:T(8,128)(2,1)} %bitcast.15), kind=kLoop, calls=%fused_computation.4 | loop fusion | flops 20971520 | bytes 20971520 | tf_op jit(solution)/shard_map/concatenate | solution.py:73
  526.9 21.9 %gather_fusion = bf16[2048,2048]{1,0:T(8,128)(2,1)} fusion(bf16[2560,2048]{1,0:T(8,128)(2,1)} %pad_maximum_fusion, s32[2048]{0:T(1024)S(1)} %broadcast_clamp_fusion), kind=kCustom, calls=%fused_computation | custom fusion | bytes 16785408 | tf_op jit(solution)/shard_map/gather | solution.py:77
  548.8 12.2 %fusion = bf16[256,2048]{1,0:T(8,128)(2,1)} fusion(bf16[2048,2048]{1,0:T(8,128)(2,1)} %gather_fusion, f32[256,8]{1,0:T(8,128)S(1)} %copy.28), kind=kLoop, calls=%fused_computation.3 | loop fusion | flops 12058624 | bytes 9445376 | tf_op jit(solution)/shard_map/reduce_sum | solution.py:79
  (46 shorter events, 3.2 us)
Async XLA Ops:
  6.5 46.7 %copy-start = (bf16[256,2048]{1,0:T(8,128)(2,1)S(1)}, bf16[256,2048]{1,0:T(8,128)(2,1)}, u32[]{:S(2)}) copy-start(bf16[256,2048]{1,0:T(8,128)(2,1)} %param.5) | copy-start | bytes 3145732
  6.5 35.2 %copy-start.3 = (bf16[2,768,256]{2,1,0:T(8,128)(2,1)S(1)}, bf16[2,768,256]{2,1,0:T(8,128)(2,1)}, u32[]{:S(2)}) copy-start(bf16[2,768,256]{2,1,0:T(8,128)(2,1)} %param.9) | copy-start | bytes 2359300
  6.5 36.1 %copy-start.5 = (s32[256,8]{0,1:T(8,128)S(1)}, s32[256,8]{0,1:T(8,128)}, u32[]{:S(2)}) copy-start(s32[256,8]{0,1:T(8,128)} %param.6) | copy-start | bytes 24580
  6.5 35.1 %all-gather.11.cloned.1.call-start = ((), (), s32[]{:S(2)}) async-start(), calls=%async_computation.3 | async-start | bytes 2359296 | tf_op jit(solution)/shard_map/all_gather | solution.py:20
  9.3 68.3 %all-gather.13.cloned.1.call-start = ((), (), s32[]{:S(2)}) async-start(), calls=%async_computation.4 | async-start | bytes 2359296 | tf_op jit(solution)/shard_map/all_gather | solution.py:20
  10.1 244.3 %all-gather.15.cloned.1.call-start = ((), (), s32[]{:S(2)}) async-start(), calls=%async_computation.5 | async-start | bytes 7864320 | tf_op jit(solution)/shard_map/all_gather | solution.py:20
  41.6 227.7 %all-gather.17.cloned.1.call-start = ((), (), s32[]{:S(2)}) async-start(), calls=%async_computation.6 | async-start | bytes 3538944 | tf_op jit(solution)/shard_map/all_gather | solution.py:64
  71.1 173.2 %all-to-all-start = ((bf16[32,80,2048]{2,1,0:T(8,128)(2,1)}), bf16[32,80,2048]{2,1,0:T(8,128)(2,1)}, u32[]{:S(2)}, u32[]{:S(2)}) async-start(bf16[32,80,2048]{2,1,0:T(8,128)(2,1)} %bitcast.57), calls=%async_computation | async-start | bytes 20971520 | tf_op jit(solution)/shard_map/all_to_all | solution.py:48
  77.5 260.4 %all-gather.19.cloned.1.call-start = ((), (), s32[]{:S(2)}) async-start(), calls=%async_computation.7 | async-start | bytes 7864320 | tf_op jit(solution)/shard_map/all_gather | solution.py:20
  78.1 338.1 %all-gather.21.cloned.1.call-start = ((), (), s32[]{:S(2)}) async-start(), calls=%async_computation.8 | async-start | bytes 3538944 | tf_op jit(solution)/shard_map/all_gather | solution.py:64
  254.4 4.3 copy-start.2
  280.2 61.3 %slice-start = ((s8[5242880]{0:T(1024)(128)(4,1)}), s8[1048576]{0:T(1024)(128)(4,1)S(1)}, s32[]{:S(2)}) async-start(s8[5242880]{0:T(1024)(128)(4,1)} %bitcast.62), calls=%async_computation.9 | async-start | bytes 2097152
  280.2 146.8 %all-to-all-start.1 = ((bf16[16,80,2048]{2,1,0:T(8,128)(2,1)}), bf16[16,80,2048]{2,1,0:T(8,128)(2,1)}, u32[]{:S(2)}, u32[]{:S(2)}) async-start(bf16[16,80,2048]{2,1,0:T(8,128)(2,1)} %bitcast.66), calls=%async_computation.1 | async-start | bytes 10485760 | tf_op jit(solution)/shard_map/all_to_all | solution.py:61
  337.9 4.0 slice-start.1
  427.0 7.5 %copy-start.4 = (f32[256,8]{0,1:T(8,128)S(1)}, f32[256,8]{0,1:T(8,128)}, u32[]{:S(2)}) copy-start(f32[256,8]{0,1:T(8,128)} %param.7) | copy-start | bytes 24580
  427.0 87.1 %all-to-all-start.2 = ((bf16[16,80,2048]{2,1,0:T(8,128)(2,1)}), bf16[16,80,2048]{2,1,0:T(8,128)(2,1)}, u32[]{:S(2)}, u32[]{:S(2)}) async-start(bf16[16,80,2048]{2,1,0:T(8,128)(2,1)} %bitcast.67), calls=%async_computation.2 | async-start | bytes 10485760 | tf_op jit(solution)/shard_map/all_to_all | solution.py:61
  526.9 34.2 %copy-start.1 = (bf16[256,2048]{1,0:T(8,128)(2,1)S(1)}, bf16[256,2048]{1,0:T(8,128)(2,1)}, u32[]{:S(2)}) copy-start(bf16[256,2048]{1,0:T(8,128)(2,1)} %param.5) | copy-start | bytes 3145732
Sparse Core Ops, SparseCore 0:
  9.4 32.1 all-gather.10
  43.3 30.5 all-gather.12
  75.5 65.7 all-gather.14
  143.3 99.1 all-gather.16
  244.0 93.8 all-gather.18
  340.0 76.2 all-gather.20
where the time goes:
time: 576 us; the launch traced here: 568 us
  waiting for transfers between devices  390 us (68%)
  local copies, waits for them, and re-layouts  62.9 us (11%)
  matrix products  42.8 us (7%)
  other arithmetic  34.6 us (6%)
  starting transfers between devices  23.7 us (4%)
  between operations  13.9 us (2%)
    all_to_all x1, waiting for transfers between devices, shards(): lax.all_to_all(send_buffer, 'expert', split_axis=0, concat_axis=1, tiled=...  166 us
    all_gather x4, waiting for transfers between devices, gather_in_order(): pieces = lax.all_gather(pieces, axes[k])  80.1 us
    all_to_all x2, waiting for transfers between devices, shards(): lax.all_to_all(jnp.dot(hidden, lax.all_gather(w_down[local_expert], DP, a...  79.5 us
    all_gather x2, waiting for transfers between devices, shards(): lax.all_gather(w_down[local_expert], DP, axis=1, tiled=True)  63.8 us
    gather x1, local copies, waits for them, and re-layouts, shards(): gathered = returned[source_rows].reshape(tok_rows, top_count, model_width)  21.9 us
    dot_general x2, matrix products, shards(): jnp.dot(hidden, lax.all_gather(w_down[local_expert], DP, axis=1, tiled=Tr...  21.7 us
    dot_general x2, matrix products, shards(): jnp.dot(rows_in, whole_of(w_gate_up[local_expert], DP, (0, 1), 0), prefer...  21.1 us
    scatter x1, local copies, waits for them, and re-layouts, shards(): jnp.zeros((experts * capacity, model_width), jnp.bfloat16).at[target]  17.9 us
  transfers between devices with their start and end apart: 9, of which 5 were waited for; matrix products, arithmetic and copies ran while one was open for 16% of the time, Pallas kernels for 0%

commit v1 on v0

--- a/solution.py
+++ b/solution.py
@@ -61,7 +61,12 @@
             lax.all_to_all(
                 jnp.dot(
                     hidden,
-                    lax.all_gather(w_down[local_expert], DP, axis=1, tiled=True),
+                    jnp.concatenate(
+                        lax.all_to_all(
+                            jnp.stack([w_down[local_expert]] * lax.axis_size(DP)), DP, 0, 0
+                        ),
+                        axis=1,
+                    ),
                     preferred_element_type=jnp.float32,
                 ).astype(jnp.bfloat16),
                 "expert",

time: 576 us -> 594 us (1.031)
  the two profiles are of different devices: /device:TPU:49 before, /device:TPU:119 now
where the time goes in v1:
time: 594 us; the launch traced here: 586 us
  waiting for transfers between devices  389 us (65%)
  local copies, waits for them, and re-layouts  67.7 us (11%)
  matrix products  41.4 us (7%)
  starting transfers between devices  39.4 us (7%)
  other arithmetic  34.6 us (6%)
  between operations  13.6 us (2%)
    all_to_all x1, waiting for transfers between devices, shards(): lax.all_to_all(send_buffer, 'expert', split_axis=0, concat_axis=1, tiled=...  170 us
    all_to_all x2, waiting for transfers between devices, shards(): lax.all_to_all(jnp.dot(hidden, jnp.concatenate(lax.all_to_all(jnp.stack([...  135 us
    all_to_all x2, waiting for transfers between devices, shards(): lax.all_to_all(jnp.stack([w_down[local_expert]] * lax.axis_size(DP)), DP,...  53.2 us
    all_gather x4, waiting for transfers between devices, gather_in_order(): pieces = lax.all_gather(pieces, axes[k])  29.8 us
    dot_general x2, matrix products, shards(): jnp.dot(rows_in, whole_of(w_gate_up[local_expert], DP, (0, 1), 0), prefer...  22.6 us
    gather x1, local copies, waits for them, and re-layouts, shards(): gathered = returned[source_rows].reshape(tok_rows, top_count, model_width)  21.9 us
    all_to_all x2, starting transfers between devices, shards(): lax.all_to_all(jnp.stack([w_down[local_expert]] * lax.axis_size(DP)), DP,...  19.4 us
    dot_general x2, matrix products, shards(): jnp.dot(hidden, jnp.concatenate(lax.all_to_all(jnp.stack([w_down[local_ex...  18.8 us
  transfers between devices with their start and end apart: 9, of which 6 were waited for; matrix products, arithmetic and copies ran while one was open for 16% of the time, Pallas kernels for 0%

profile of v1, /device:TPU:119, one launch (start us, length us, event | category | flops | bytes accessed | tf_op | source)
XLA Modules:
  0.0 585.6 jit_solution(609043987441414186)
XLA Ops:
  6.5 2.7 fusion.21
  10.1 29.7 %all-gather.7.cloned.1.call-done = bf16[2,256,1536]{2,1,0:T(8,128)(2,1)} async-done(((bf16[1,256,1536]{2,1,0:T(8,128)(2,1)}), bf16[2,256,1536]{2,1,0:T(8,128)(2,1)}) %all-gather.7.cloned.1.call-update) | async-done | bytes 1572880 | tf_op jit(solution)/shard_map/all_gather | solution.py:20
  40.4 9.1 %reduce-window.6 = s32[32,16,128]{2,1,0:T(8,128)S(1)} reduce-window(s32[32,16,128]{2,1,0:T(8,128)S(1)} %fusion.14, s32[]{:T(128)} %constant.38.clone.1), window={size=1x1x128 pad=0_0x0_0x127_0}, to_apply=%region_0.0 | reduce-window | flops 8323072 | bytes 524292 | tf_op jit(solution)/shard_map/reduce-window
  50.4 17.9 %scatter_custom_fusion = bf16[2560,2048]{1,0:T(8,128)(2,1)} fusion(s32[2048]{0:T(1024)S(1)} %bitcast.79, bf16[]{:T(256)} %constant.36.clone.1, bf16[256,2048]{1,0:T(8,128)(2,1)S(1)} %copy-done), kind=kCustom, calls=%fused_computation.5 | custom fusion | bytes 11534338 | tf_op jit(solution)/shard_map/scatter | solution.py:46
  68.3 6.3 %all-to-all-start = ((bf16[32,80,2048]{2,1,0:T(8,128)(2,1)}), bf16[32,80,2048]{2,1,0:T(8,128)(2,1)}, u32[]{:S(2)}, u32[]{:S(2)}) async-start(bf16[32,80,2048]{2,1,0:T(8,128)(2,1)} %bitcast.63), calls=%async_computation | async-start | bytes 20971520 | tf_op jit(solution)/shard_map/all_to_all | solution.py:48
  75.4 169.7 %all-to-all-done = bf16[32,80,2048]{2,1,0:T(8,128)(2,1)} async-done(((bf16[32,80,2048]{2,1,0:T(8,128)(2,1)}), bf16[32,80,2048]{2,1,0:T(8,128)(2,1)}, u32[]{:S(2)}, u32[]{:S(2)}) %all-to-all-start) | async-done | bytes 10485792 | tf_op jit(solution)/shard_map/all_to_all | solution.py:48
  247.0 13.1 %all-to-all-start.1 = ((bf16[8,768,256]{1,2,0:T(8,128)(2,1)}), bf16[8,768,256]{1,2,0:T(8,128)(2,1)}, u32[]{:S(2)}, u32[]{:S(2)}) async-start(bf16[8,768,256]{1,2,0:T(8,128)(2,1)} %stack.6), calls=%async_computation.1 | async-start | bytes 6291456 | tf_op jit(solution)/shard_map/all_to_all | solution.py:65
  260.2 10.2 %fusion.20 = (bf16[1,16,80,2048]{3,2,0,1:T(8,128)(2,1)}, bf16[1,16,80,2048]{3,2,0,1:T(8,128)(2,1)}) fusion(bf16[2,16,80,2048]{3,2,0,1:T(8,128)(2,1)} %bitcast.8), kind=kLoop, calls=%fused_computation.41 | loop fusion | bytes 20971520 | tf_op jit(solution)/shard_map/slice | solution.py:51
  270.4 5.8 copy.30
  276.3 30.4 %all-to-all-done.1 = bf16[8,768,256]{1,2,0:T(8,128)(2,1)} async-done(((bf16[8,768,256]{1,2,0:T(8,128)(2,1)}), bf16[8,768,256]{1,2,0:T(8,128)(2,1)}, u32[]{:S(2)}, u32[]{:S(2)}) %all-to-all-start.1) | async-done | bytes 3145760 | tf_op jit(solution)/shard_map/all_to_all | solution.py:65
  308.5 6.4 %all-to-all-start.3 = ((bf16[8,768,256]{1,2,0:T(8,128)(2,1)}), bf16[8,768,256]{1,2,0:T(8,128)(2,1)}, u32[]{:S(2)}, u32[]{:S(2)}) async-start(bf16[8,768,256]{1,2,0:T(8,128)(2,1)} %stack.7), calls=%async_computation.3 | async-start | bytes 6291456 | tf_op jit(solution)/shard_map/all_to_all | solution.py:65
  314.9 12.1 %fusion.22 = f32[1280,1536]{1,0:T(8,128)S(1)} fusion(bf16[1280,2048]{1,0:T(8,128)(2,1)} %bitcast.71, bf16[2048,1536]{1,0:T(8,128)(2,1)} %bitcast.66), kind=kOutput, calls=%fused_computation.43 | convolution fusion | flops 8053063680 | bytes 19398656 | tf_op jit(solution)/shard_map/dot_general | solution.py:52
  327.0 8.0 %convolution_convert_fusion.1 = bf16[1280,2048]{1,0:T(8,128)(2,1)} fusion(bf16[768,2048]{0,1:T(8,128)(2,1)} %bitcast.15, f32[1280,1536]{1,0:T(8,128)S(1)} %fusion.22), kind=kOutput, calls=%fused_computation.8 | convolution fusion | flops 4035051520 | bytes 16252928 | tf_op jit(solution)/shard_map/dot_general | solution.py:62
  334.9 22.8 %all-to-all-done.3 = bf16[8,768,256]{1,2,0:T(8,128)(2,1)} async-done(((bf16[8,768,256]{1,2,0:T(8,128)(2,1)}), bf16[8,768,256]{1,2,0:T(8,128)(2,1)}, u32[]{:S(2)}, u32[]{:S(2)}) %all-to-all-start.3) | async-done | bytes 3145760 | tf_op jit(solution)/shard_map/all_to_all | solution.py:65
  357.8 8.0 %all-to-all-start.2 = ((bf16[16,80,2048]{2,1,0:T(8,128)(2,1)}), bf16[16,80,2048]{2,1,0:T(8,128)(2,1)}, u32[]{:S(2)}, u32[]{:S(2)}) async-start(bf16[16,80,2048]{2,1,0:T(8,128)(2,1)} %bitcast.72), calls=%async_computation.2 | async-start | bytes 10485760 | tf_op jit(solution)/shard_map/all_to_all | solution.py:61
  365.8 3.6 copy.32
  369.8 10.6 %fusion.23 = f32[1280,1536]{1,0:T(8,128)} fusion(bf16[1280,2048]{1,0:T(8,128)(2,1)S(1)} %bitcast.70, bf16[2048,1536]{1,0:T(8,128)(2,1)S(1)} %bitcast.67), kind=kOutput, calls=%fused_computation.44 | convolution fusion | flops 8053063680 | bytes 19398656 | tf_op jit(solution)/shard_map/dot_general | solution.py:52
  380.3 10.9 %convolution_convert_fusion = bf16[1280,2048]{1,0:T(8,128)(2,1)} fusion(bf16[768,2048]{0,1:T(8,128)(2,1)} %bitcast.25, f32[1280,1536]{1,0:T(8,128)} %fusion.23), kind=kOutput, calls=%fused_computation.7 | convolution fusion | flops 4035051520 | bytes 16252928 | tf_op jit(solution)/shard_map/dot_general | solution.py:62
  391.2 54.7 %all-to-all-done.2 = bf16[16,80,2048]{2,1,0:T(8,128)(2,1)} async-done(((bf16[16,80,2048]{2,1,0:T(8,128)(2,1)}), bf16[16,80,2048]{2,1,0:T(8,128)(2,1)}, u32[]{:S(2)}, u32[]{:S(2)}) %all-to-all-start.2) | async-done | bytes 5242912 | tf_op jit(solution)/shard_map/all_to_all | solution.py:61
  445.9 5.6 all-to-all-start.4
  451.6 80.4 %all-to-all-done.4 = bf16[16,80,2048]{2,1,0:T(8,128)(2,1)} async-done(((bf16[16,80,2048]{2,1,0:T(8,128)(2,1)}), bf16[16,80,2048]{2,1,0:T(8,128)(2,1)}, u32[]{:S(2)}, u32[]{:S(2)}) %all-to-all-start.4) | async-done | bytes 5242912 | tf_op jit(solution)/shard_map/all_to_all | solution.py:61
  532.0 12.7 %pad_maximum_fusion = bf16[2560,2048]{1,0:T(8,128)(2,1)} fusion(bf16[1280,2048]{1,0:T(8,128)(2,1)} %bitcast.27, bf16[1280,2048]{1,0:T(8,128)(2,1)} %bitcast.17), kind=kLoop, calls=%fused_computation.4 | loop fusion | flops 20971520 | bytes 20971520 | tf_op jit(solution)/shard_map/concatenate | solution.py:78
  544.7 21.9 %gather_fusion = bf16[2048,2048]{1,0:T(8,128)(2,1)} fusion(bf16[2560,2048]{1,0:T(8,128)(2,1)} %pad_maximum_fusion, s32[2048]{0:T(1024)S(1)} %broadcast_clamp_fusion), kind=kCustom, calls=%fused_computation | custom fusion | bytes 16785408 | tf_op jit(solution)/shard_map/gather | solution.py:82
  566.6 12.2 %fusion = bf16[256,2048]{1,0:T(8,128)(2,1)} fusion(bf16[2048,2048]{1,0:T(8,128)(2,1)} %gather_fusion, f32[256,8]{1,0:T(8,128)S(1)} %copy.34), kind=kLoop, calls=%fused_computation.3 | loop fusion | flops 12058624 | bytes 9445376 | tf_op jit(solution)/shard_map/reduce_sum | solution.py:84
  (46 shorter events, 7.4 us)
Async XLA Ops:
  6.5 43.8 %copy-start = (bf16[256,2048]{1,0:T(8,128)(2,1)S(1)}, bf16[256,2048]{1,0:T(8,128)(2,1)}, u32[]{:S(2)}) copy-start(bf16[256,2048]{1,0:T(8,128)(2,1)} %param.5) | copy-start | bytes 3145732
  6.5 33.3 %copy-start.4 = (s32[256,8]{0,1:T(8,128)S(1)}, s32[256,8]{0,1:T(8,128)}, u32[]{:S(2)}) copy-start(s32[256,8]{0,1:T(8,128)} %param.6) | copy-start | bytes 24580
  6.5 33.3 %all-gather.7.cloned.1.call-start = ((), (), s32[]{:S(2)}) async-start(), calls=%async_computation.5 | async-start | bytes 2359296 | tf_op jit(solution)/shard_map/all_gather | solution.py:20
  9.3 65.3 %all-gather.9.cloned.1.call-start = ((), (), s32[]{:S(2)}) async-start(), calls=%async_computation.6 | async-start | bytes 2359296 | tf_op jit(solution)/shard_map/all_gather | solution.py:20
  10.0 260.4 %all-gather.11.cloned.1.call-start = ((), (), s32[]{:S(2)}) async-start(), calls=%async_computation.7 | async-start | bytes 7864320 | tf_op jit(solution)/shard_map/all_gather | solution.py:20
  68.3 6.9 %copy-start.2 = (bf16[2,768,256]{2,1,0:T(8,128)(2,1)S(1)}, bf16[2,768,256]{2,1,0:T(8,128)(2,1)}, u32[]{:S(2)}) copy-start(bf16[2,768,256]{2,1,0:T(8,128)(2,1)} %param.9) | copy-start | bytes 2359300
  68.3 176.8 %all-to-all-start = ((bf16[32,80,2048]{2,1,0:T(8,128)(2,1)}), bf16[32,80,2048]{2,1,0:T(8,128)(2,1)}, u32[]{:S(2)}, u32[]{:S(2)}) async-start(bf16[32,80,2048]{2,1,0:T(8,128)(2,1)} %bitcast.63), calls=%async_computation | async-start | bytes 20971520 | tf_op jit(solution)/shard_map/all_to_all | solution.py:48
  74.6 291.2 %all-gather.13.cloned.1.call-start = ((), (), s32[]{:S(2)}) async-start(), calls=%async_computation.8 | async-start | bytes 7864320 | tf_op jit(solution)/shard_map/all_gather | solution.py:20
  247.0 59.7 %all-to-all-start.1 = ((bf16[8,768,256]{1,2,0:T(8,128)(2,1)}), bf16[8,768,256]{1,2,0:T(8,128)(2,1)}, u32[]{:S(2)}, u32[]{:S(2)}) async-start(bf16[8,768,256]{1,2,0:T(8,128)(2,1)} %stack.6), calls=%async_computation.1 | async-start | bytes 6291456 | tf_op jit(solution)/shard_map/all_to_all | solution.py:65
  308.5 49.2 %all-to-all-start.3 = ((bf16[8,768,256]{1,2,0:T(8,128)(2,1)}), bf16[8,768,256]{1,2,0:T(8,128)(2,1)}, u32[]{:S(2)}, u32[]{:S(2)}) async-start(bf16[8,768,256]{1,2,0:T(8,128)(2,1)} %stack.7), calls=%async_computation.3 | async-start | bytes 6291456 | tf_op jit(solution)/shard_map/all_to_all | solution.py:65
  357.8 11.6 %slice-start = ((s8[5242880]{0:T(1024)(128)(4,1)}), s8[1048576]{0:T(1024)(128)(4,1)S(1)}, s32[]{:S(2)}) async-start(s8[5242880]{0:T(1024)(128)(4,1)} %bitcast.68), calls=%async_computation.9 | async-start | bytes 2097152
  357.8 88.1 %all-to-all-start.2 = ((bf16[16,80,2048]{2,1,0:T(8,128)(2,1)}), bf16[16,80,2048]{2,1,0:T(8,128)(2,1)}, u32[]{:S(2)}, u32[]{:S(2)}) async-start(bf16[16,80,2048]{2,1,0:T(8,128)(2,1)} %bitcast.72), calls=%async_computation.2 | async-start | bytes 10485760 | tf_op jit(solution)/shard_map/all_to_all | solution.py:61
  365.8 4.0 slice-start.1
  445.9 5.6 copy-start.3
  445.9 86.1 %all-to-all-start.4 = ((bf16[16,80,2048]{2,1,0:T(8,128)(2,1)}), bf16[16,80,2048]{2,1,0:T(8,128)(2,1)}, u32[]{:S(2)}, u32[]{:S(2)}) async-start(bf16[16,80,2048]{2,1,0:T(8,128)(2,1)} %bitcast.73), calls=%async_computation.4 | async-start | bytes 10485760 | tf_op jit(solution)/shard_map/all_to_all | solution.py:61
  544.7 34.2 %copy-start.1 = (bf16[256,2048]{1,0:T(8,128)(2,1)S(1)}, bf16[256,2048]{1,0:T(8,128)(2,1)}, u32[]{:S(2)}) copy-start(bf16[256,2048]{1,0:T(8,128)(2,1)} %param.5) | copy-start | bytes 3145732
Sparse Core Ops, SparseCore 0:
  9.4 30.3 all-gather.6
  41.5 30.5 all-gather.8
  73.8 65.4 all-gather.10
  140.7 66.2 all-gather.12
